TPU v7x, 32 devices: a whole 2x2x4 slice. The times are simulated.
32 devices in a mesh: row: 8 (over z, x), col: 4 (over y, core).
Axes of the slice: x: 2, y: 2, z: 4, core: 2. Of those that a mesh axis runs over, the one named last changes fastest.
Arguments:
- innovations: float32 [64, 16384], P(None, ('row', 'col')), may hold values from -300 to 300
- obs_factors: float32 [64, 16384], P(None, ('row', 'col')), may hold values from -6 to 6
- component: int32 [16384], P(('row', 'col')), may hold values 0 or 1
- obs_error: float32 [16384], P(('row', 'col')), may hold values from 0.5 to 2
- coupling: float32 [2, 2], replicated, may hold values from 0.5 to 2
- tile_slots: int32 [8, 4, 8, 3], P('row', 'col'), may hold values from 0 to 7, as said below
Outputs:
- increment: float32 [64, 16384], P(None, ('row', 'col'))
- residual: float32 [64, 16384], P(None, ('row', 'col'))
Inputs may be any that keep to these rules, and one draw needn't show every extreme that they name: `tile_slots`: each device's slots name distinct (local block row, local block column) pairs; on some device all 8 slots are live; the live flag is 0 or 1; local block rows are below 4 and local block columns below 8.
All inputs are finite; a program needn't handle non-finite values. No bound on the sum of `component` on one device may be relied on, other than what follows from the above.
Results may differ from a plain program's by a relative error of at most 0.0003.
Values sent between devices are 32-bit elements; how exact they have to be, the bound alone decides.
A program may use at most 64 MiB of HBM per device.

v0:
```python
import functools

import jax
import jax.numpy as jnp
from jax import lax
from jax.experimental import pallas as pl
from jax.experimental.pallas import tpu as pltpu
from jax.sharding import PartitionSpec as P

ITERS = 3
length_sq = 12.0
MESH = pl.DeviceIdType.MESH
VMEM = pl.BlockSpec(memory_space=pltpu.VMEM)
SMEM = pl.BlockSpec(memory_space=pltpu.SMEM)


def peers(rows, cols):
    r, c = lax.axis_index("row"), lax.axis_index("col")
    to_col = [(r, lax.rem(c + k, cols)) for k in range(1, cols)]
    to_row = [(lax.rem(r + k, rows), c) for k in range(1, rows)]
    from_col = [lax.rem(c + cols - k, cols) for k in range(1, cols)]
    from_row = [lax.rem(r + rows - k, rows) for k in range(1, rows)]
    return r, c, to_col, to_row, from_col, from_row


def greet(devices):
    barrier = pltpu.get_barrier_semaphore()
    for device in devices:
        pl.semaphore_signal(barrier, inc=1, device_id=device, device_id_type=MESH)
    pl.semaphore_wait(barrier, len(devices))


def remote(src, dst, send, recv, device):
    return pltpu.make_async_remote_copy(
        src_ref=src, dst_ref=dst, send_sem=send, recv_sem=recv,
        device_id=device, device_id_type=MESH,
    )


def legs(rows):
    outer = 4 if rows % 4 == 0 else rows
    order = sorted(range(1, outer), key=lambda k: (abs(2 * k - outer), k))
    return outer, rows // outer, order


def gather_kernel(rows, cols, x, s, by_col, by_row, total, s1, s2, part,
                  send_c, recv_c, send_z, recv_z, send_x, recv_x,
                  send_1, recv_1, send_2, recv_2, own):
    r, c, to_col, to_row, from_col, from_row = peers(rows, cols)
    outer, inner, order = legs(rows)
    z, w = lax.div(r, inner), lax.rem(r, inner)
    greet(to_col + to_row)
    small = [remote(s, s1.at[c], send_1.at[k], recv_1.at[k], d) for k, d in enumerate(to_col)]
    for copy in small:
        copy.start()
    to_z = {k: (lax.rem(z + k, outer) * inner + w, c) for k in order}
    to_x = {j: (z * inner + lax.rem(w + j, inner), c) for j in range(1, inner)}
    from_z = {k: lax.rem(z + outer - k, outer) for k in [0] + order}
    from_x = {j: lax.rem(w + inner - j, inner) for j in range(1, inner)}

    def along(k, slot):
        return remote(x, by_row.at[slot], send_z.at[k - 1], recv_z.at[k - 1], to_z[k])

    def across(k, j, slot):
        source = x if k == 0 else by_row.at[slot]
        return remote(source, by_row.at[slot], send_x.at[k, j - 1], recv_x.at[k, j - 1], to_x[j])

    bulk = [along(k, r) for k in order]
    bulk += [across(0, j, r) for j in to_x]
    bulk += [remote(x, by_col.at[c], send_c.at[k], recv_c.at[k], d) for k, d in enumerate(to_col)]
    for copy in bulk:
        copy.start()
    keep = [
        pltpu.make_async_copy(x, by_col.at[c], own.at[0]),
        pltpu.make_async_copy(x, by_row.at[r], own.at[1]),
        pltpu.make_async_copy(s, s1.at[c], own.at[2]),
    ]
    for copy in keep:
        copy.start()
    keep[2].wait()
    for k, q in enumerate(from_col):
        remote(s, s1.at[q], send_1.at[k], recv_1.at[k], to_col[k]).wait_recv()
    part[...] = jnp.sum(s1[...], axis=0)
    second = [remote(part, s2.at[r], send_2.at[k], recv_2.at[k], d) for k, d in enumerate(to_row)]
    for copy in second:
        copy.start()
    mine = pltpu.make_async_copy(part, s2.at[r], own.at[3])
    mine.start()
    for k in order:
        slot = from_z[k] * inner + w
        along(k, slot).wait_recv()
        for j in to_x:
            copy = across(k, j, slot)
            copy.start()
            bulk.append(copy)
    for k, q in enumerate(from_col):
        remote(x, by_col.at[q], send_c.at[k], recv_c.at[k], to_col[k]).wait_recv()
    for k in [0] + order:
        for j in to_x:
            across(k, j, from_z[k] * inner + from_x[j]).wait_recv()
    for k, q in enumerate(from_row):
        remote(part, s2.at[q], send_2.at[k], recv_2.at[k], to_row[k]).wait_recv()
    mine.wait()
    keep[0].wait()
    keep[1].wait()
    total[...] = jnp.sum(s2[...], axis=0)
    for copy in small + bulk + second:
        copy.wait_send()


def scatter_kernel(rows, cols, by_col, by_row, s, out, total, got_c, got_z, got_x, stage,
                   s1, s2, part, send_c, recv_c, send_z, recv_z, send_x, recv_x,
                   send_1, recv_1, send_2, recv_2, own):
    r, c, to_col, to_row, from_col, from_row = peers(rows, cols)
    outer, inner, order = legs(rows)
    z, w = lax.div(r, inner), lax.rem(r, inner)
    greet(to_col + to_row)
    small = [remote(s, s1.at[c], send_1.at[k], recv_1.at[k], d) for k, d in enumerate(to_col)]
    for copy in small:
        copy.start()
    across = {}
    for k in order + [0]:
        for j in range(1, inner):
            side = lax.rem(w + j, inner)
            across[k, j] = remote(
                by_row.at[lax.rem(z + k, outer) * inner + side], got_x.at[k, j - 1],
                send_x.at[k, j - 1], recv_x.at[k, j - 1], (z * inner + side, c),
            )
            across[k, j].start()
    flat = [remote(by_col.at[d[1]], got_c.at[k], send_c.at[k], recv_c.at[k], d)
            for k, d in enumerate(to_col)]
    for copy in flat:
        copy.start()
    keep = pltpu.make_async_copy(s, s1.at[c], own.at[0])
    keep.start()
    keep.wait()
    for k, q in enumerate(from_col):
        remote(s, s1.at[q], send_1.at[k], recv_1.at[k], to_col[k]).wait_recv()
    part[...] = jnp.sum(s1[...], axis=0)
    second = [remote(part, s2.at[r], send_2.at[k], recv_2.at[k], d) for k, d in enumerate(to_row)]
    for copy in second:
        copy.start()
    mine = pltpu.make_async_copy(part, s2.at[r], own.at[1])
    mine.start()

    def joined(k):
        value = by_row[lax.rem(z + k, outer) * inner + w]
        for j in range(1, inner):
            across[k, j].wait_recv()
            value = value + got_x[k, j - 1]
        return value

    along = []
    for k in order:
        stage[k - 1] = joined(k)
        copy = remote(stage.at[k - 1], got_z.at[k - 1], send_z.at[k - 1], recv_z.at[k - 1],
                      (lax.rem(z + k, outer) * inner + w, c))
        copy.start()
        along.append(copy)
    for copy in flat:
        copy.wait_recv()
    out[...] = joined(0) + (by_col[c] + jnp.sum(got_c[...], axis=0))
    for copy in along:
        copy.wait_recv()
    out[...] += jnp.sum(got_z[...], axis=0)
    for k, q in enumerate(from_row):
        remote(part, s2.at[q], send_2.at[k], recv_2.at[k], to_row[k]).wait_recv()
    mine.wait()
    total[...] = jnp.sum(s2[...], axis=0)
    for copy in small + flat + along + second + list(across.values()):
        copy.wait_send()


def semaphores(rows, cols):
    outer, inner, order = legs(rows)
    sides = (outer, max(inner - 1, 1))
    shapes = [(cols - 1,)] * 2 + [(outer - 1,)] * 2 + [sides] * 2
    shapes += [(cols - 1,)] * 2 + [(rows - 1,)] * 2 + [(4,)]
    return [pltpu.SemaphoreType.DMA(shape) for shape in shapes]


def small_scratch(rows, cols):
    return [
        pltpu.VMEM((cols, 8, 128), jnp.float32),
        pltpu.VMEM((rows, 8, 128), jnp.float32),
        pltpu.VMEM((8, 128), jnp.float32),
    ]


def gather(x, s, rows, cols, number):
    f32 = jnp.float32
    return pl.pallas_call(
        functools.partial(gather_kernel, rows, cols),
        out_shape=(
            jax.ShapeDtypeStruct((cols,) + x.shape, f32),
            jax.ShapeDtypeStruct((rows,) + x.shape, f32),
            jax.ShapeDtypeStruct((8, 128), f32),
        ),
        in_specs=[VMEM] * 2,
        out_specs=(VMEM,) * 3,
        scratch_shapes=small_scratch(rows, cols) + semaphores(rows, cols),
        compiler_params=pltpu.CompilerParams(collective_id=number, has_side_effects=True),
    )(x, s)


def scatter(by_col, by_row, s, number):
    f32 = jnp.float32
    cols, rows = by_col.shape[0], by_row.shape[0]
    block = by_col.shape[1:]
    outer, inner, order = legs(rows)
    return pl.pallas_call(
        functools.partial(scatter_kernel, rows, cols),
        out_shape=(jax.ShapeDtypeStruct(block, f32), jax.ShapeDtypeStruct((8, 128), f32)),
        in_specs=[VMEM] * 3,
        out_specs=(VMEM,) * 2,
        scratch_shapes=[
            pltpu.VMEM((cols - 1,) + block, f32),
            pltpu.VMEM((outer - 1,) + block, f32),
            pltpu.VMEM((outer, max(inner - 1, 1)) + block, f32),
            pltpu.VMEM((outer - 1,) + block, f32),
        ] + small_scratch(rows, cols) + semaphores(rows, cols),
        compiler_params=pltpu.CompilerParams(collective_id=number, has_side_effects=True),
    )(by_col, by_row, s)


def build_kernel(depth, slots, by_col, by_row, coupling, high, low):
    number = pl.program_id(0)
    a, b = slots[number, 0], slots[number, 1]

    @pl.when(slots[number, 2] > 0)
    def _():
        left = jnp.transpose(by_col[a, :depth + 8])
        left, left_label = left[:, :depth], left[:, depth:depth + 1]
        right, right_label = by_row[b, :depth], by_row[b, depth:depth + 1]
        left_norm = jnp.sum(left * left, axis=1, keepdims=True)
        right_norm = jnp.sum(right * right, axis=0, keepdims=True)
        products = jnp.dot(
            left, right, precision=lax.Precision.HIGHEST, preferred_element_type=jnp.float32
        )
        ocean = right_label > 0.5
        first = jnp.where(ocean, coupling[0, 1], coupling[0, 0])
        second = jnp.where(ocean, coupling[1, 1], coupling[1, 0])
        pair = jnp.where(left_label > 0.5, second, first)
        tile = pair * jnp.exp(-(left_norm + right_norm - 2.0 * products) / length_sq)
        top = tile.astype(jnp.bfloat16)
        high[0] = top
        low[0] = (tile - top.astype(jnp.float32)).astype(jnp.bfloat16)


def build(depth, slots, by_col, by_row, coupling):
    count, tile = slots.shape[0], by_col.shape[2]
    stored = jax.ShapeDtypeStruct((count, tile, tile), jnp.bfloat16)
    return pl.pallas_call(
        functools.partial(build_kernel, depth),
        grid=(count,),
        out_shape=(stored, stored),
        in_specs=[SMEM, VMEM, VMEM, SMEM],
        out_specs=(pl.BlockSpec((1, tile, tile), lambda i: (i, 0, 0)),) * 2,
    )(slots, by_col, by_row, coupling)


def times(values, high, low, side):
    dims = (((1,), (side,)), ((), ()))
    n = values.shape[0]
    top = values.astype(jnp.bfloat16).astype(jnp.float32)
    both = jnp.concatenate([top, values - top], axis=0).astype(jnp.bfloat16)
    wide = lax.dot_general(both, high, dims, preferred_element_type=jnp.float32)
    rest = lax.dot_general(
        top.astype(jnp.bfloat16), low, dims, preferred_element_type=jnp.float32
    )
    return wide[:n] + (wide[n:] + rest)


def fold(x):
    total = x[:, :128]
    for start in range(128, x.shape[1], 128):
        total = total + x[:, start:start + 128]
    return total


def sweep_kernel(rhs, start, slots, row_values, column_values, high, low,
                 row_image, column_image, dots):
    number = pl.program_id(0)
    a, b = slots[number, 0], slots[number, 1]
    kept = row_image.shape[1]
    weigh = kept > rhs

    @pl.when(number == 0)
    def _():
        row_image[...] = jnp.zeros_like(row_image)
        column_image[...] = jnp.zeros_like(column_image)
        dots[...] = jnp.zeros_like(dots)

    @pl.when(slots[number, 2] > 0)
    def _():
        rv, cv = row_values[a, start:start + rhs], column_values[b, start:start + rhs]
        t_high, t_low = high[0], low[0]
        rows, columns = rv, cv
        if weigh:
            ones = jnp.ones((16, rv.shape[1]), jnp.float32)
            rows = jnp.concatenate([rv, ones], axis=0)
            columns = jnp.concatenate([cv, ones], axis=0)
        right_part = times(columns, t_high, t_low, 1)
        left_part = times(rows, t_high, t_low, 0)
        row_image[a] += right_part[:kept]
        column_image[b] += left_part[:kept]
        amount = 2.0 * fold(right_part[:rhs] * rv)
        if weigh:
            amount = amount + fold(right_part[rhs:rhs + 1] * (rv * rv))
            amount = amount + fold(left_part[rhs:rhs + 1] * (cv * cv))
        dots[...] += amount


def turn_kernel(rhs, slots, beta, row_fresh, column_fresh, row_old, column_old, high, low,
                row_image, column_image, dots, row_values, column_values):
    @pl.when(pl.program_id(0) == 0)
    def _():
        factor = beta[:, :1]
        start = row_old.shape[1] - rhs
        for a in range(row_old.shape[0]):
            row_values[a] = row_fresh[a] + factor * row_old[a, start:]
        for b in range(column_old.shape[0]):
            column_values[b] = column_fresh[b] + factor * column_old[b, start:]

    sweep_kernel(rhs, 0, slots, row_values, column_values, high, low,
                 row_image, column_image, dots)


def turn(rhs, slots, beta, row_fresh, column_fresh, row_old, column_old, high, low):
    count, tile = high.shape[0], high.shape[1]
    whole = lambda shape: pl.BlockSpec(shape, lambda i: (0,) * len(shape))
    tiles = pl.BlockSpec((1, tile, tile), lambda i: (i, 0, 0))
    shapes = (row_fresh.shape, column_fresh.shape, (rhs, 128), row_fresh.shape, column_fresh.shape)
    return pl.pallas_call(
        functools.partial(turn_kernel, rhs),
        grid=(count,),
        out_shape=tuple(jax.ShapeDtypeStruct(shape, jnp.float32) for shape in shapes),
        in_specs=[SMEM] + [VMEM] * 5 + [tiles, tiles],
        out_specs=tuple(whole(shape) for shape in shapes),
    )(slots, beta, row_fresh, column_fresh, row_old, column_old, high, low)


def sweep(rhs, start, kept, slots, row_values, column_values, high, low):
    count, tile = high.shape[0], high.shape[1]
    whole = lambda shape: pl.BlockSpec(shape, lambda i: (0,) * len(shape))
    tiles = pl.BlockSpec((1, tile, tile), lambda i: (i, 0, 0))
    shapes = (
        (row_values.shape[0], kept, tile), (column_values.shape[0], kept, tile), (rhs, 128)
    )
    return pl.pallas_call(
        functools.partial(sweep_kernel, rhs, start),
        grid=(count,),
        out_shape=tuple(jax.ShapeDtypeStruct(shape, jnp.float32) for shape in shapes),
        in_specs=[SMEM, VMEM, VMEM, tiles, tiles],
        out_specs=tuple(whole(shape) for shape in shapes),
    )(slots, row_values, column_values, high, low)


def spread(sums):
    return jnp.pad(sums[None, :], ((0, 7), (0, 128 - sums.shape[0])))


def shards(rows, cols, innovations, obs_factors, component, obs_error, coupling, tile_slots):
    slots = tile_slots[0, 0]
    rhs = innovations.shape[0]
    depth = obs_factors.shape[0]
    labels = jnp.pad(component.astype(jnp.float32)[None, :], ((0, 7), (0, 0)))
    packed = jnp.concatenate([obs_factors, labels, innovations], axis=0)
    by_col, by_row, total = gather(
        packed, spread(jnp.sum(innovations * innovations, axis=1)), rows, cols, 0
    )
    norm_now = total[0, :rhs]

    high, low = build(depth, slots, by_col, by_row, coupling)
    row_values, column_values = by_col, by_row

    increment = jnp.zeros_like(innovations)
    residual = innovations
    direction = innovations
    diagonal = None
    for repeat in range(ITERS):
        if repeat == 0:
            row_image, column_image, dots = sweep(
                rhs, depth + 8, rhs + 8, slots, by_col, by_row, high, low
            )
            own = obs_error
        else:
            row_image, column_image, dots, row_values, column_values = turn(
                rhs, slots, jnp.broadcast_to(beta, (rhs, 128)), by_col, by_row,
                row_values, column_values, high, low,
            )
            own = diagonal
        part = jnp.sum(dots, axis=1) + jnp.sum(own[None, :] * direction * direction, axis=1)
        product, total = scatter(row_image, column_image, spread(part), 1 if repeat == 0 else 2)
        if repeat == 0:
            diagonal = obs_error + product[rhs]
        image = diagonal[None, :] * direction + product[:rhs]
        alpha = norm_now / total[0, :rhs]
        increment = increment + alpha[:, None] * direction
        residual = residual - alpha[:, None] * image
        if repeat + 1 < ITERS:
            by_col, by_row, total = gather(
                residual, spread(jnp.sum(residual * residual, axis=1)), rows, cols, 3
            )
            norm_next = total[0, :rhs]
            beta = (norm_next / norm_now)[:, None]
            direction = residual + beta * direction
            norm_now = norm_next
    return (increment, residual)


def solution(mesh):
    return jax.shard_map(
        functools.partial(shards, mesh.shape["row"], mesh.shape["col"]),
        mesh=mesh,
        in_specs=(
            P(None, ("row", "col")),
            P(None, ("row", "col")),
            P(("row", "col")),
            P(("row", "col")),
            P(),
            P("row", "col", None, None),
        ),
        out_specs=(P(None, ("row", "col")), P(None, ("row", "col"))),
        check_vma=False,
    )
```

profile of v0, /device:TPU:0, one launch (start us, length us, event | category | flops | bytes accessed | tf_op | source)
XLA Modules:
  0.0 231.2 jit_solution(9362498718393622775)
XLA Ops:
  0.6 1.0 fusion.8
  1.7 0.7 convert_element_type.12
  3.0 1.3 copy.12
  4.3 1.7 fusion.x
  6.0 47.5 %shard_map.77 = (f32[4,136,512]{2,1,0:T(8,128)}, f32[8,136,512]{2,1,0:T(8,128)}, f32[8,128]{1,0:T(8,128)}) custom-call(f32[136,512]{1,0:T(8,128)} %fusion.x, f32[8,128]{1,0:T(8,128)} %pad.24.s), custom_call_target="tpu_custom_call" | custom-call | tf_op jit(solution)/shard_map/pallas_call | solution.py:192
  53.5 10.6 %shard_map.78 = (bf16[8,512,512]{2,1,0:T(8,128)(2,1)}, bf16[8,512,512]{2,1,0:T(8,128)(2,1)}) custom-call(s32[8,3]{1,0:T(8,128)} %bitcast.22, f32[4,136,512]{2,1,0:T(8,128)} %get-tuple-element.31.by_col.row_values.row_old, f32[8,136,512]{2,1,0:T(8,128)} %get-tuple-element.32.by_row.column_values.column_old, f32[2,2]{1,0:T(2,128)} %coupling.1), custom_call_target="tpu_custom_call" | custom-call | tf_op jit(solution)/shard_map/pallas_call | solution.py:253
  64.2 9.6 %shard_map.79 = (f32[4,72,512]{2,1,0:T(8,128)}, f32[8,72,512]{2,1,0:T(8,128)}, f32[64,128]{1,0:T(8,128)}) custom-call(s32[8,3]{1,0:T(8,128)} %bitcast.23, f32[4,136,512]{2,1,0:T(8,128)} %get-tuple-element.31.by_col.row_values.row_old, f32[8,136,512]{2,1,0:T(8,128)} %get-tuple-element.32.by_row.column_values.column_old, ...), custom_call_target="tpu_custom_call" | custom-call | tf_op jit(solution)/shard_map/pallas_call | solution.py:350
  73.7 0.9 reduce_sum.82
  75.2 25.6 %shard_map.80 = (f32[72,512]{1,0:T(8,128)}, f32[8,128]{1,0:T(8,128)}) custom-call(f32[4,72,512]{2,1,0:T(8,128)} %get-tuple-element.35.by_col, f32[8,72,512]{2,1,0:T(8,128)} %get-tuple-element.36.by_row, f32[8,128]{1,0:T(8,128)} %pad.25.s), custom_call_target="tpu_custom_call" | custom-call | tf_op jit(solution)/shard_map/pallas_call | solution.py:211
  100.8 0.7 fusion.9
  101.5 0.7 slice.26
  102.2 1.7 multiply_reduce_fusion.1
  104.0 0.6 pad.26.s
  104.6 25.0 %shard_map.81 = (f32[4,64,512]{2,1,0:T(8,128)}, f32[8,64,512]{2,1,0:T(8,128)}, f32[8,128]{1,0:T(8,128)}) custom-call(f32[64,512]{1,0:T(8,128)} %get-tuple-element.65.x, f32[8,128]{1,0:T(8,128)} %pad.26.s), custom_call_target="tpu_custom_call" | custom-call | tf_op jit(solution)/shard_map/pallas_call | solution.py:192
  129.6 0.7 divide_bitcast_fusion.1
  130.3 0.7 broadcast_in_dim.15.beta
  131.0 10.9 %shard_map.82 = (f32[4,64,512]{2,1,0:T(8,128)}, f32[8,64,512]{2,1,0:T(8,128)}, f32[64,128]{1,0:T(8,128)}, f32[4,64,512]{2,1,0:T(8,128)}, f32[8,64,512]{2,1,0:T(8,128)}) custom-call(s32[8,3]{1,0:T(8,128)} %bitcast.24, f32[64,128]{1,0:T(8,128)} %broadcast_in_dim.15.beta, f32[4,64,512]{2,1,0:T(8,128)} %get-tuple-element.41.row_fresh, ...), custom_call_target="tpu_custom_call" | custom-call | tf_op jit(solution)/shard_map/pallas_call | solution.py:334
  141.9 0.9 reduce_sum.85
  143.6 21.2 %shard_map.83 = (f32[64,512]{1,0:T(8,128)}, f32[8,128]{1,0:T(8,128)}) custom-call(f32[4,64,512]{2,1,0:T(8,128)} %get-tuple-element.43.by_col, f32[8,64,512]{2,1,0:T(8,128)} %get-tuple-element.44.by_row, f32[8,128]{1,0:T(8,128)} %pad.27.s), custom_call_target="tpu_custom_call" | custom-call | tf_op jit(solution)/shard_map/pallas_call | solution.py:211
  164.8 0.7 fusion.10
  165.5 1.7 multiply_reduce_fusion
  167.2 0.6 pad.28.s
  167.9 24.8 %shard_map.84 = (f32[4,64,512]{2,1,0:T(8,128)}, f32[8,64,512]{2,1,0:T(8,128)}, f32[8,128]{1,0:T(8,128)}) custom-call(f32[64,512]{1,0:T(8,128)} %get-tuple-element.61.x, f32[8,128]{1,0:T(8,128)} %pad.28.s), custom_call_target="tpu_custom_call" | custom-call | tf_op jit(solution)/shard_map/pallas_call | solution.py:192
  192.6 0.7 divide_bitcast_fusion
  193.3 1.1 fusion.5
  194.4 0.7 broadcast_in_dim.17.beta
  195.1 10.2 %shard_map.85 = (f32[4,64,512]{2,1,0:T(8,128)}, f32[8,64,512]{2,1,0:T(8,128)}, f32[64,128]{1,0:T(8,128)}, f32[4,64,512]{2,1,0:T(8,128)}, f32[8,64,512]{2,1,0:T(8,128)}) custom-call(s32[8,3]{1,0:T(8,128)} %bitcast.25, f32[64,128]{1,0:T(8,128)} %broadcast_in_dim.17.beta, f32[4,64,512]{2,1,0:T(8,128)} %get-tuple-element.49.row_fresh, ...), custom_call_target="tpu_custom_call" | custom-call | tf_op jit(solution)/shard_map/pallas_call | solution.py:334
  205.4 0.9 reduce_sum.88
  206.3 0.6 pad.29.s
  206.9 21.9 %shard_map.86 = (f32[64,512]{1,0:T(8,128)}, f32[8,128]{1,0:T(8,128)}) custom-call(f32[4,64,512]{2,1,0:T(8,128)} %get-tuple-element.53.by_col, f32[8,64,512]{2,1,0:T(8,128)} %get-tuple-element.54.by_row, f32[8,128]{1,0:T(8,128)} %pad.29.s), custom_call_target="tpu_custom_call" | custom-call | tf_op jit(solution)/shard_map/pallas_call | solution.py:211
  228.8 0.7 fusion.11
  229.5 1.7 fusion.7
  (16 shorter events, 2.0 us)
Async XLA Ops:
  64.2 38.1 %copy-start.3 = (f32[512]{0:T(512)S(1)}, f32[512]{0:T(512)}, u32[]{:S(2)}) copy-start(f32[512]{0:T(512)} %param.9) | copy-start | bytes 6148
  64.2 38.1 %copy-start = (f32[64,512]{1,0:T(8,128)S(1)}, f32[64,512]{1,0:T(8,128)}, u32[]{:S(2)}) copy-start(f32[64,512]{1,0:T(8,128)} %param.6) | copy-start | bytes 393220
  131.0 11.8 %copy-start.1 = (f32[64,512]{1,0:T(8,128)S(1)}, f32[64,512]{1,0:T(8,128)}, u32[]{:S(2)}) copy-start(f32[64,512]{1,0:T(8,128)} %get-tuple-element.65.x) | copy-start | bytes 393220
  195.1 34.3 %copy-start.2 = (f32[64,512]{1,0:T(8,128)S(1)}, f32[64,512]{1,0:T(8,128)}, u32[]{:S(2)}) copy-start(f32[64,512]{1,0:T(8,128)} %get-tuple-element.61.x) | copy-start | bytes 393220
where the time goes:
time: 233 us; the launch traced here: 231 us
  Pallas kernels  207 us (89%)
  other arithmetic  16 us (7%)
  local copies, waits for them, and re-layouts  7.11 us (3%)
    pallas_call x3, Pallas kernels, gather(): pl.pallas_call(functools.partial(gather_kernel, rows, cols), out_shape=(j...  97.3 us
    pallas_call x3, Pallas kernels, scatter(): pl.pallas_call(functools.partial(scatter_kernel, rows, cols), out_shape=(...  68.7 us
    pallas_call x2, Pallas kernels, turn(): pl.pallas_call(functools.partial(turn_kernel, rhs), grid=(count,), out_sh...  21.2 us
    pallas_call x1, Pallas kernels, build(): pl.pallas_call(functools.partial(build_kernel, depth), grid=(count,), out...  10.6 us
    pallas_call x1, Pallas kernels, sweep(): pl.pallas_call(functools.partial(sweep_kernel, rhs, start), grid=(count,)...  9.57 us

commit v1 on v0

v1 whole, which is shorter than its diff:
```python
import functools
import math

import jax
import jax.numpy as jnp
from jax import lax
from jax.experimental import pallas as pl
from jax.experimental.pallas import tpu as pltpu
from jax.sharding import PartitionSpec as P

ITERS = 3
length_sq = 12.0
MESH = pl.DeviceIdType.MESH
VMEM = pl.BlockSpec(memory_space=pltpu.VMEM)
SMEM = pl.BlockSpec(memory_space=pltpu.SMEM)
F32, BF16 = jnp.float32, jnp.bfloat16
PIECE_FACTORS = 24
PIECE_FIRST = 24
PIECE = 16
EXTRA = 8
ONES = 16
DEAD = 1000.0


def legs(rows):
    outer = 4 if rows % 4 == 0 else rows
    return outer, rows // outer


def pieces(height, size):
    return [(start, min(size, height - start)) for start in range(0, height, size)]


def remote(src, dst, send, recv, device):
    return pltpu.make_async_remote_copy(
        src_ref=src, dst_ref=dst, send_sem=send, recv_sem=recv,
        device_id=device, device_id_type=MESH,
    )


def split2(x):
    top = x.astype(BF16)
    return top, (x - top.astype(F32)).astype(BF16)


def split3(x):
    first = x.astype(BF16)
    rest = x - first.astype(F32)
    second = rest.astype(BF16)
    return first, second, (rest - second.astype(F32)).astype(BF16)


def fold(x):
    total = x[:, :128]
    for start in range(128, x.shape[1], 128):
        total = total + x[:, start:start + 128]
    return total


def lane_sums(x):
    rest = 128 - x.shape[0]
    square = jnp.concatenate([x, jnp.zeros((rest, 128), F32)], axis=0) if rest else x
    return jnp.sum(jnp.transpose(square), axis=0, keepdims=True)


def column(row, height, width):
    square = jnp.transpose(jnp.broadcast_to(row, (128, 128)))[:height]
    return jnp.concatenate([square] * (width // 128), axis=1)


def stack_rows(values, width):
    place = lax.broadcasted_iota(jnp.int32, (16, width), 0)
    total = jnp.zeros((16, width), F32)
    for n, value in enumerate(values):
        total = jnp.where(place == n, value.astype(F32), total)
    return total.astype(BF16)


class Sends:
    def __init__(self):
        self.held = []

    def go(self, copy, when=None):
        if when is None:
            copy.start()
        else:
            pl.when(when)(copy.start)
        self.held.append((copy, when))

    def drain(self):
        for copy, when in self.held:
            if when is None:
                copy.wait_send()
            else:
                pl.when(when)(copy.wait_send)
        self.held = []


def kernel(rows, cols, innov, factors, labels, errors, coupling, slots, inc_out, res_out,
           f_row, f_col, v_row, v_col, d_row, d_col, x_row, x_col, left, t_high, t_low,
           col_part, row_part, where_slot, s1, s2,
           x_stage, x_got, z_stage, z_got, c_stage, c_got, product, diag, direction,
           gf_row, gf_col, gv_row, gv_col, hf_z, hf_x, hf_c, hv_z, hv_x, hv_c,
           rx, rz, rc, qx, qz, qc, r1, r2, q1, q2):
    r, c = lax.axis_index("row"), lax.axis_index("col")
    outer, inner = legs(rows)
    z, w = lax.div(r, inner), lax.rem(r, inner)
    has_low, has_high = z > 0, z < outer - 1
    low, high = (r - inner, c), (r + inner, c)
    to_col = [(r, lax.rem(c + k, cols)) for k in range(1, cols)]
    to_row = [(lax.rem(r + k, rows), c) for k in range(1, rows)]
    from_col = [lax.rem(c + cols - k, cols) for k in range(1, cols)]
    from_row = [lax.rem(r + rows - k, rows) for k in range(1, rows)]
    side_of = [lax.rem(w + j, inner) for j in range(1, inner)]
    back_of = [lax.rem(w + inner - j, inner) for j in range(1, inner)]
    rhs, tile = innov.shape
    depth = factors.shape[0]
    count = slots.shape[0]

    def gather_start(sends, source, row_buf, col_buf, parts, g_row, g_col, h_z, h_x, h_c):
        for n, (start, size) in enumerate(parts):
            span = pl.ds(start, size)
            mine = source.at[span]
            target = row_buf.at[r, span]
            sends.go(remote(mine, target, h_z.at[0, 0, n], g_row.at[r, n], low), has_low)
            sends.go(remote(mine, target, h_z.at[1, 0, n], g_row.at[r, n], high), has_high)
            for j, side in enumerate(side_of):
                sends.go(remote(mine, target, h_x.at[0, 0, j, n], g_row.at[r, n],
                                (z * inner + side, c)))
            for k, device in enumerate(to_col):
                sends.go(remote(mine, col_buf.at[c, span], h_c.at[k, n], g_col.at[c, n], device))

    def gather_relay(sends, row_buf, parts, g_row, h_z, h_x):
        for step in range(1, outer):
            for n, (start, size) in enumerate(parts):
                span = pl.ds(start, size)
                for way in range(2):
                    slot = r - step * inner if way else r + step * inner
                    there = z - step >= 0 if way else z + step < outer
                    onward = has_high if way else has_low
                    block = row_buf.at[slot, span]
                    arrival = remote(block, block, h_z.at[way, step, n], g_row.at[slot, n],
                                     high if way else low)
                    pl.when(there)(arrival.wait_recv)
                    sends.go(arrival, there & onward)
                    for j, side in enumerate(side_of):
                        sends.go(remote(block, block, h_x.at[way, step, j, n], g_row.at[slot, n],
                                        (z * inner + side, c)), there)
            yield step

    def gather_finish(row_buf, col_buf, parts, g_row, g_col, h_x, h_c):
        for n, (start, size) in enumerate(parts):
            span = pl.ds(start, size)
            for k, q in enumerate(from_col):
                block = col_buf.at[q, span]
                remote(block, block, h_c.at[k, n], g_col.at[q, n], to_col[k]).wait_recv()
        for n, (start, size) in enumerate(parts):
            span = pl.ds(start, size)
            for plane in range(outer):
                for j, back in enumerate(back_of):
                    slot = plane * inner + back
                    block = row_buf.at[slot, span]
                    remote(block, block, h_x.at[0, 0, j, n], g_row.at[slot, n],
                           (z * inner + back, c)).wait_recv()

    def small_start(sends, kind, value):
        s1[kind, c] = jnp.broadcast_to(value, (8, 128))
        for k, device in enumerate(to_col):
            sends.go(remote(s1.at[kind, c], s1.at[kind, c], q1.at[kind, k], r1.at[kind, k], device))

    def small_middle(sends, kind):
        for k, q in enumerate(from_col):
            remote(s1.at[kind, q], s1.at[kind, q], q1.at[kind, k], r1.at[kind, k],
                   to_col[k]).wait_recv()
        s2[kind, r] = jnp.sum(s1[kind], axis=0)
        for k, device in enumerate(to_row):
            sends.go(remote(s2.at[kind, r], s2.at[kind, r], q2.at[kind, k], r2.at[kind, k], device))

    def small_end(kind):
        for k, q in enumerate(from_row):
            remote(s2.at[kind, q], s2.at[kind, q], q2.at[kind, k], r2.at[kind, k],
                   to_row[k]).wait_recv()
        return jnp.sum(s2[kind], axis=0)[:1]

    barrier = pltpu.get_barrier_semaphore()
    for device in to_col + to_row:
        pl.semaphore_signal(barrier, inc=1, device_id=device, device_id_type=MESH)

    scale = math.sqrt(2.0 / (length_sq * math.log(2.0)))
    own = jnp.concatenate(
        [factors[...] * scale, jnp.broadcast_to(labels[...].astype(F32), (EXTRA, tile))], axis=0
    )
    f_row[r] = own
    f_col[c] = own
    start_values = innov[...]
    rr_part = lane_sums(fold(start_values * start_values))
    pl.semaphore_wait(barrier, len(to_col) + len(to_row))

    f_parts = pieces(depth + EXTRA, PIECE_FACTORS)
    v_parts = pieces(rhs, PIECE)
    sends_f, sends_v, sends_s, sends_r = Sends(), Sends(), Sends(), Sends()
    gather_start(sends_f, f_row.at[r], f_row, f_col, f_parts, gf_row, gf_col, hf_z, hf_x, hf_c)
    small_start(sends_s, 0, rr_part)
    gather_start(sends_v, innov, v_row.at[0], v_col.at[0], v_parts,
                 gv_row, gv_col, hv_z, hv_x, hv_c)

    v_row[0, r] = start_values
    v_col[0, c] = start_values
    direction[...] = start_values
    inc_out[...] = jnp.zeros_like(start_values)
    res_out[...] = start_values
    for part in (col_part, row_part):
        part[count] = jnp.zeros(part.shape[1:], F32)

    def locate(n, carry):
        a, b = lax.div(n, rows), lax.rem(n, rows)
        found = jnp.int32(count)
        for s in range(count):
            hit = (slots[s, 2] > 0) & (slots[s, 0] == a) & (slots[s, 1] == b)
            found = jnp.where(hit, s, found)
        where_slot[n] = found
        return carry

    lax.fori_loop(0, rows * cols, locate, 0)

    logs = [[jnp.log(jnp.full((1, tile), coupling[i, j], F32)) * (1.0 / math.log(2.0))
             for j in range(2)] for i in range(2)]
    one = jnp.ones((1, tile), F32)
    nothing = jnp.zeros((tile - 6 * depth - 16, tile), BF16)

    relay_f = gather_relay(sends_f, f_row, f_parts, gf_row, hf_z, hf_x)
    next(relay_f)
    small_middle(sends_s, 0)
    for n, (start, size) in enumerate(f_parts):
        for k, q in enumerate(from_col):
            block = f_col.at[q, pl.ds(start, size)]
            remote(block, block, hf_c.at[k, n], gf_col.at[q, n], to_col[k]).wait_recv()

    def prepare(a, carry):
        g = f_col[a, :depth]
        label = f_col[a, depth:depth + 1]
        g1, g2, g3 = split3(g)
        m = split3(-0.5 * jnp.sum(g * g, axis=0, keepdims=True))
        extra = stack_rows(list(m) + [one] * 3 + [label] * 3, tile)
        stack = jnp.concatenate([g1, g1, g2, g2, g1, g3, extra, nothing], axis=0)
        left[a] = jnp.transpose(stack)
        return carry

    lax.fori_loop(0, cols, prepare, 0)
    for _ in relay_f:
        pass
    for n, (start, size) in enumerate(f_parts):
        span = pl.ds(start, size)
        for plane in range(outer):
            for j, back in enumerate(back_of):
                slot = plane * inner + back
                block = f_row.at[slot, span]
                remote(block, block, hf_x.at[0, 0, j, n], gf_row.at[slot, n],
                       (z * inner + back, c)).wait_recv()

    def build(s, carry):
        a, b = slots[s, 0], slots[s, 1]
        g = f_row[b, :depth]
        label = f_row[b, depth:depth + 1]
        g1, g2, g3 = split3(g)
        gone = jnp.where(slots[s, 2] > 0, 0.0, DEAD)
        base = -0.5 * jnp.sum(g * g, axis=0, keepdims=True)
        base = base + (logs[0][0] + label * (logs[0][1] - logs[0][0])) - gone
        slope = (logs[1][0] - logs[0][0]) + label * (
            (logs[1][1] - logs[1][0]) - (logs[0][1] - logs[0][0]))
        extra = stack_rows([one] * 3 + list(split3(base)) + list(split3(slope)), tile)
        stack = jnp.concatenate([g1, g2, g1, g2, g3, g1, extra, nothing], axis=0)
        value = jnp.exp2(jnp.dot(left[a], stack, preferred_element_type=F32))
        top, rest = split2(value)
        t_high[s] = top
        t_low[s] = rest
        return carry

    relay_v = gather_relay(sends_v, v_row.at[0], v_parts, gv_row, hv_z, hv_x)
    half = count // 2
    lax.fori_loop(0, half, build, 0)
    next(relay_v)
    lax.fori_loop(half, count, build, 0)
    for _ in relay_v:
        pass
    gather_finish(v_row.at[0], v_col.at[0], v_parts, gv_row, gv_col, hv_x, hv_c)
    norm_now = small_end(0)
    sends_f.drain()

    ones_rows = jnp.ones((ONES, tile), BF16)
    bottom = rhs + ONES

    def put(target, index, value):
        top, rest = split2(value)
        target[index, :rhs] = top
        target[index, rhs:bottom] = ones_rows
        target[index, bottom:] = rest

    def sweep(s, carry):
        a, b = slots[s, 0], slots[s, 1]
        for values, index, side, part in ((x_row, b, 1, row_part), (x_col, a, 0, col_part)):
            dims = (((1,), (side,)), ((), ()))
            wide = lax.dot_general(values[index], t_high[s], dims, preferred_element_type=F32)
            rest = lax.dot_general(values[index, :bottom], t_low[s], dims,
                                   preferred_element_type=F32)
            part[s, :rhs] = wide[:rhs] + (wide[bottom:] + rest[:rhs])
            part[s, rhs:] = wide[rhs:rhs + EXTRA] + rest[rhs:rhs + EXTRA]
        return carry

    def column_image(b, span):
        total = col_part[where_slot[b], span]
        for a in range(1, cols):
            total = total + col_part[where_slot[a * rows + b], span]
        return total

    def row_image(a, span):
        total = row_part[where_slot[a * rows], span]
        for b in range(1, rows):
            total = total + row_part[where_slot[a * rows + b], span]
        return total

    order = []
    lower_half = z < outer // 2
    for i in range(outer - 1):
        down = outer - 1 - i
        order.append(jnp.where(lower_half, jnp.where(down <= z, down - 1, down),
                               jnp.where(i >= z, i + 1, i)))
    order.append(z)

    for repeat in range(ITERS):
        first = repeat == 0
        if first:
            def ready_row(b, carry):
                put(x_row, b, v_row[0, b])
                return carry

            def ready_col(a, carry):
                put(x_col, a, v_col[0, a])
                return carry
        else:
            old_row = v_row.at[0] if repeat == 1 else d_row
            old_col = v_col.at[0] if repeat == 1 else d_col
            weight = column(beta, rhs, tile)

            def ready_row(b, carry):
                value = v_row[repeat, b] + weight * old_row[b]
                d_row[b] = value
                put(x_row, b, value)
                return carry

            def ready_col(a, carry):
                value = v_col[repeat, a] + weight * old_col[a]
                d_col[a] = value
                put(x_col, a, value)
                return carry

        lax.fori_loop(0, rows, ready_row, 0)
        lax.fori_loop(0, cols, ready_col, 0)
        lax.fori_loop(0, count, sweep, 0)

        held_col = v_col.at[0] if first else d_col
        held_row = v_row.at[0] if first else d_row
        parts = pieces(rhs + EXTRA, PIECE_FIRST) if first else pieces(rhs, PIECE)
        sends_r.drain()
        sends_s.drain()

        def send_across(i):
            for j, side in enumerate(side_of):
                for n, (start, size) in enumerate(parts):
                    span = pl.ds(start, size)
                    x_stage[i, j, span] = column_image(order[i] * inner + side, span)
                    sends_r.go(remote(x_stage.at[i, j, span], x_got.at[i, j, span],
                                      qx.at[i, j, n], rx.at[i, j, n], (z * inner + side, c)))

        def joined(i, n, span):
            value = column_image(order[i] * inner + w, span)
            for j in range(inner - 1):
                block = x_got.at[i, j, span]
                remote(block, block, qx.at[i, j, n], rx.at[i, j, n],
                       (z * inner + side_of[j], c)).wait_recv()
                value = value + x_got[i, j, span]
            return value

        send_across(0)
        own_err = errors[...] if first else diag[...]
        here = direction[...]
        dots = fold(own_err * here * here)
        for k in range(cols):
            a = to_col[k][1] if k < cols - 1 else c
            for n, (start, size) in enumerate(parts):
                span = pl.ds(start, size)
                value = row_image(a, span)
                c_stage[k, span] = value
                if k < cols - 1:
                    sends_r.go(remote(c_stage.at[k, span], c_got.at[k, span],
                                      qc.at[k, n], rc.at[k, n], to_col[k]))
            held = held_col[a]
            dots = dots + 2.0 * fold(c_stage[k, :rhs] * held)
            if first:
                dots = dots + fold(c_stage[k, rhs:rhs + 1] * (held * held))
        if first:
            def weigh(b, carry):
                held = held_row[b]
                return carry + fold(column_image(b, pl.ds(rhs, EXTRA))[:1] * (held * held))

            dots = lax.fori_loop(0, rows, weigh, dots)
        small_start(sends_s, 1, lane_sums(dots))
        for i in range(1, outer):
            send_across(i)
        small_middle(sends_s, 1)

        for i in range(outer - 1):
            q = order[i]
            below = q < z
            way = jnp.where(below, 0, 1)
            more = jnp.where(below, z + 1 < outer, z > 0)
            target = (jnp.where(below, r - inner, r + inner), c)
            for n, (start, size) in enumerate(parts):
                span = pl.ds(start, size)
                z_stage[i, span] = joined(i, n, span)
                copy = remote(z_stage.at[i, span], z_got.at[way, q, span],
                              qz.at[i, n], rz.at[way, q, n], target)

                @pl.when(more)
                def _():
                    copy.wait_recv()
                    z_stage[i, span] += z_got[way, q, span]

                sends_r.go(copy)
        for n, (start, size) in enumerate(parts):
            span = pl.ds(start, size)
            for k, q in enumerate(from_col):
                block = c_got.at[k, span]
                remote(block, block, qc.at[k, n], rc.at[k, n], to_col[k]).wait_recv()
            value = c_stage[cols - 1, span]
            for k in range(cols - 1):
                value = value + c_got[k, span]
            product[span] = value + joined(outer - 1, n, span)
            for way, there in enumerate((has_high, has_low)):
                @pl.when(there)
                def _():
                    block = z_got.at[way, z, span]
                    remote(block, block, qz.at[0, n], rz.at[way, z, n],
                           high if way == 0 else low).wait_recv()
                    product[span] += z_got[way, z, span]
        alpha = norm_now / small_end(1)
        step = column(alpha, rhs, tile)
        if first:
            diag[...] = errors[...] + product[rhs:rhs + 1]
        image = diag[...] * here + product[:rhs]
        inc_out[...] += step * here
        residual = res_out[...] - step * image
        res_out[...] = residual
        sends_v.drain()
        if repeat + 1 < ITERS:
            v_row[repeat + 1, r] = residual
            v_col[repeat + 1, c] = residual
            row_buf, col_buf = v_row.at[repeat + 1], v_col.at[repeat + 1]
            gather_start(sends_v, row_buf.at[r], row_buf, col_buf, v_parts,
                         gv_row, gv_col, hv_z, hv_x, hv_c)
            sends_s.drain()
            small_start(sends_s, 0, lane_sums(fold(residual * residual)))
            relay = gather_relay(sends_v, row_buf, v_parts, gv_row, hv_z, hv_x)
            next(relay)
            small_middle(sends_s, 0)
            for _ in relay:
                pass
            gather_finish(row_buf, col_buf, v_parts, gv_row, gv_col, hv_x, hv_c)
            norm_next = small_end(0)
            beta = norm_next / norm_now
            norm_now = norm_next
            direction[...] = residual + column(beta, rhs, tile) * here
    sends_r.drain()
    sends_s.drain()
    sends_v.drain()


def shards(rows, cols, innovations, obs_factors, component, obs_error, coupling, tile_slots):
    slots = tile_slots[0, 0]
    rhs, tile = innovations.shape
    depth = obs_factors.shape[0]
    count = slots.shape[0]
    outer, inner = legs(rows)
    sides = max(inner - 1, 1)
    tall, wide = depth + EXTRA, rhs + EXTRA
    nf = len(pieces(tall, PIECE_FACTORS))
    nv = len(pieces(rhs, PIECE))
    nr = max(len(pieces(wide, PIECE_FIRST)), nv)
    dma = pltpu.SemaphoreType.DMA
    scratch = [
        pltpu.VMEM((rows, tall, tile), F32),
        pltpu.VMEM((cols, tall, tile), F32),
        pltpu.VMEM((ITERS, rows, rhs, tile), F32),
        pltpu.VMEM((ITERS, cols, rhs, tile), F32),
        pltpu.VMEM((rows, rhs, tile), F32),
        pltpu.VMEM((cols, rhs, tile), F32),
        pltpu.VMEM((rows, 2 * rhs + ONES, tile), BF16),
        pltpu.VMEM((cols, 2 * rhs + ONES, tile), BF16),
        pltpu.VMEM((cols, tile, tile), BF16),
        pltpu.VMEM((count, tile, tile), BF16),
        pltpu.VMEM((count, tile, tile), BF16),
        pltpu.VMEM((count + 1, wide, tile), F32),
        pltpu.VMEM((count + 1, wide, tile), F32),
        pltpu.SMEM((rows * cols,), jnp.int32),
        pltpu.VMEM((2, cols, 8, 128), F32),
        pltpu.VMEM((2, rows, 8, 128), F32),
        pltpu.VMEM((outer, sides, wide, tile), F32),
        pltpu.VMEM((outer, sides, wide, tile), F32),
        pltpu.VMEM((outer, wide, tile), F32),
        pltpu.VMEM((2, outer, wide, tile), F32),
        pltpu.VMEM((cols, wide, tile), F32),
        pltpu.VMEM((cols, wide, tile), F32),
        pltpu.VMEM((wide, tile), F32),
        pltpu.VMEM((1, tile), F32),
        pltpu.VMEM((rhs, tile), F32),
        dma((rows, nf)), dma((cols, nf)), dma((rows, nv)), dma((cols, nv)),
        dma((2, outer, nf)), dma((2, outer, sides, nf)), dma((cols, nf)),
        dma((2, outer, nv)), dma((2, outer, sides, nv)), dma((cols, nv)),
        dma((outer, sides, nr)), dma((2, outer, nr)), dma((cols, nr)),
        dma((outer, sides, nr)), dma((outer, nr)), dma((cols, nr)),
        dma((2, cols)), dma((2, rows)), dma((2, cols)), dma((2, rows)),
    ]
    out = jax.ShapeDtypeStruct((rhs, tile), F32)
    return pl.pallas_call(
        functools.partial(kernel, rows, cols),
        out_shape=(out, out),
        in_specs=[VMEM] * 4 + [SMEM] * 2,
        out_specs=(VMEM, VMEM),
        scratch_shapes=scratch,
        compiler_params=pltpu.CompilerParams(collective_id=0, has_side_effects=True),
    )(innovations, obs_factors, component.reshape(1, tile), obs_error.reshape(1, tile),
      coupling, slots)


def solution(mesh):
    return jax.shard_map(
        functools.partial(shards, mesh.shape["row"], mesh.shape["col"]),
        mesh=mesh,
        in_specs=(
            P(None, ("row", "col")),
            P(None, ("row", "col")),
            P(("row", "col")),
            P(("row", "col")),
            P(),
            P("row", "col", None, None),
        ),
        out_specs=(P(None, ("row", "col")), P(None, ("row", "col"))),
        check_vma=False,
    )
```

time: 233 us -> 152 us (0.65)
  Pallas kernels: 207 us -> 147 us
  other arithmetic: 16 us -> 0 us
  local copies, waits for them, and re-layouts: 7.11 us -> 3.61 us
    pallas_call x10 -> x1, Pallas kernels: 207 us -> 147 us  [shards(): pl.pallas_call(functools.partial(kernel, rows, cols), out_shape=(out, out...]
    reduce_sum x8 -> x0, other arithmetic: 8.4 us -> none  [the longest x2 3.49 us: shards(): jnp.sum(residual * residual, axis=1)]
    pad x6 -> x0, local copies, waits for them, and re-layouts: 3.63 us -> none  [spread(): return jnp.pad(sums[None, :], ((0, 7), (0, 128 - sums.shape[0])))]
    div x5 -> x0, other arithmetic: 3.48 us -> none  [the longest x3 2.09 us: shards(): alpha = norm_now / total[0, :rhs]]
    unnamed x8 -> x6, local copies, waits for them, and re-layouts: 0.01 us -> 2.94 us
where the time goes in v1:
time: 152 us; the launch traced here: 151 us
  Pallas kernels  147 us (97%)
  local copies, waits for them, and re-layouts  3.61 us (2%)
    pallas_call x1, Pallas kernels, shards(): pl.pallas_call(functools.partial(kernel, rows, cols), out_shape=(out, out...  147 us

profile of v1, /device:TPU:0, one launch (start us, length us, event | category | flops | bytes accessed | tf_op | source)
XLA Modules:
  0.0 151.4 jit_solution(6114722805223026209)
XLA Ops:
  0.6 0.0 copy-start.1
  0.6 0.7 copy-done.1
  1.3 0.7 copy.9
  2.0 147.1 %shard_map.77 = (f32[64,512]{1,0:T(8,128)}, f32[64,512]{1,0:T(8,128)}) custom-call(f32[64,512]{1,0:T(8,128)} %innov.1, f32[64,512]{1,0:T(8,128)} %factors.1, s32[1,512]{1,0:T(1,128)} %bitcast.4, f32[1,512]{1,0:T(1,128)} %bitcast.5, f32[2,2]{1,0:T(2,128)} %coupling.1, s32[8,3]{1,0:T(8,128)} %bitcast.3), custom_call_target="tpu_custom_call" | custom-call | tf_op jit(solution)/shard_map/pallas_call | solution.py:524
  149.1 0.0 copy-start
  149.1 1.6 %copy.12 = f32[64,512]{1,0:T(8,128)} copy(f32[64,512]{1,0:T(8,128)} %get-tuple-element.4) | data formatting | bytes 262144
  150.7 0.0 copy-done
  150.7 0.7 copy.13
Async XLA Ops:
  0.6 0.7 copy-start.1
  149.1 1.6 %copy-start = (f32[64,512]{1,0:T(8,128)S(1)}, f32[64,512]{1,0:T(8,128)}, u32[]{:S(2)}) copy-start(f32[64,512]{1,0:T(8,128)} %get-tuple-element.5) | copy-start | bytes 393220

commit v2 on v1

--- a/solution.py
+++ b/solution.py
@@ -148,39 +148,47 @@
                                         (z * inner + side, c)), there)
             yield step
 
-    def gather_finish(row_buf, col_buf, parts, g_row, g_col, h_x, h_c):
+    def gather_cols(col_buf, parts, g_col, h_c):
         for n, (start, size) in enumerate(parts):
-            span = pl.ds(start, size)
             for k, q in enumerate(from_col):
-                block = col_buf.at[q, span]
+                block = col_buf.at[q, pl.ds(start, size)]
                 remote(block, block, h_c.at[k, n], g_col.at[q, n], to_col[k]).wait_recv()
+
+    def gather_rows(row_buf, parts, g_row, h_x):
         for n, (start, size) in enumerate(parts):
-            span = pl.ds(start, size)
             for plane in range(outer):
                 for j, back in enumerate(back_of):
                     slot = plane * inner + back
-                    block = row_buf.at[slot, span]
+                    block = row_buf.at[slot, pl.ds(start, size)]
                     remote(block, block, h_x.at[0, 0, j, n], g_row.at[slot, n],
                            (z * inner + back, c)).wait_recv()
 
     def small_start(sends, kind, value):
         s1[kind, c] = jnp.broadcast_to(value, (8, 128))
+        mine = s1.at[kind, c, pl.ds(0, 1)]
         for k, device in enumerate(to_col):
-            sends.go(remote(s1.at[kind, c], s1.at[kind, c], q1.at[kind, k], r1.at[kind, k], device))
+            sends.go(remote(mine, mine, q1.at[kind, k], r1.at[kind, k], device))
 
     def small_middle(sends, kind):
         for k, q in enumerate(from_col):
-            remote(s1.at[kind, q], s1.at[kind, q], q1.at[kind, k], r1.at[kind, k],
-                   to_col[k]).wait_recv()
-        s2[kind, r] = jnp.sum(s1[kind], axis=0)
+            there = s1.at[kind, q, pl.ds(0, 1)]
+            remote(there, there, q1.at[kind, k], r1.at[kind, k], to_col[k]).wait_recv()
+        total = s1[kind, 0, :1]
+        for k in range(1, cols):
+            total = total + s1[kind, k, :1]
+        s2[kind, r] = jnp.broadcast_to(total, (8, 128))
+        mine = s2.at[kind, r, pl.ds(0, 1)]
         for k, device in enumerate(to_row):
-            sends.go(remote(s2.at[kind, r], s2.at[kind, r], q2.at[kind, k], r2.at[kind, k], device))
+            sends.go(remote(mine, mine, q2.at[kind, k], r2.at[kind, k], device))
 
     def small_end(kind):
         for k, q in enumerate(from_row):
-            remote(s2.at[kind, q], s2.at[kind, q], q2.at[kind, k], r2.at[kind, k],
-                   to_row[k]).wait_recv()
-        return jnp.sum(s2[kind], axis=0)[:1]
+            there = s2.at[kind, q, pl.ds(0, 1)]
+            remote(there, there, q2.at[kind, k], r2.at[kind, k], to_row[k]).wait_recv()
+        total = s2[kind, 0, :1]
+        for k in range(1, rows):
+            total = total + s2[kind, k, :1]
+        return total
 
     barrier = pltpu.get_barrier_semaphore()
     for device in to_col + to_row:
@@ -199,8 +207,8 @@
     f_parts = pieces(depth + EXTRA, PIECE_FACTORS)
     v_parts = pieces(rhs, PIECE)
     sends_f, sends_v, sends_s, sends_r = Sends(), Sends(), Sends(), Sends()
+    small_start(sends_s, 0, rr_part)
     gather_start(sends_f, f_row.at[r], f_row, f_col, f_parts, gf_row, gf_col, hf_z, hf_x, hf_c)
-    small_start(sends_s, 0, rr_part)
     gather_start(sends_v, innov, v_row.at[0], v_col.at[0], v_parts,
                  gv_row, gv_col, hv_z, hv_x, hv_c)
 
@@ -231,10 +239,7 @@
     relay_f = gather_relay(sends_f, f_row, f_parts, gf_row, hf_z, hf_x)
     next(relay_f)
     small_middle(sends_s, 0)
-    for n, (start, size) in enumerate(f_parts):
-        for k, q in enumerate(from_col):
-            block = f_col.at[q, pl.ds(start, size)]
-            remote(block, block, hf_c.at[k, n], gf_col.at[q, n], to_col[k]).wait_recv()
+    gather_cols(f_col, f_parts, gf_col, hf_c)
 
     def prepare(a, carry):
         g = f_col[a, :depth]
@@ -249,14 +254,9 @@
     lax.fori_loop(0, cols, prepare, 0)
     for _ in relay_f:
         pass
-    for n, (start, size) in enumerate(f_parts):
-        span = pl.ds(start, size)
-        for plane in range(outer):
-            for j, back in enumerate(back_of):
-                slot = plane * inner + back
-                block = f_row.at[slot, span]
-                remote(block, block, hf_x.at[0, 0, j, n], gf_row.at[slot, n],
-                       (z * inner + back, c)).wait_recv()
+    relay = gather_relay(sends_v, v_row.at[0], v_parts, gv_row, hv_z, hv_x)
+    next(relay)
+    gather_rows(f_row, f_parts, gf_row, hf_x)
 
     def build(s, carry):
         a, b = slots[s, 0], slots[s, 1]
@@ -276,16 +276,10 @@
         t_low[s] = rest
         return carry
 
-    relay_v = gather_relay(sends_v, v_row.at[0], v_parts, gv_row, hv_z, hv_x)
     half = count // 2
     lax.fori_loop(0, half, build, 0)
-    next(relay_v)
+    next(relay)
     lax.fori_loop(half, count, build, 0)
-    for _ in relay_v:
-        pass
-    gather_finish(v_row.at[0], v_col.at[0], v_parts, gv_row, gv_col, hv_x, hv_c)
-    norm_now = small_end(0)
-    sends_f.drain()
 
     ones_rows = jnp.ones((ONES, tile), BF16)
     bottom = rhs + ONES
@@ -296,16 +290,19 @@
         target[index, rhs:bottom] = ones_rows
         target[index, bottom:] = rest
 
-    def sweep(s, carry):
-        a, b = slots[s, 0], slots[s, 1]
-        for values, index, side, part in ((x_row, b, 1, row_part), (x_col, a, 0, col_part)):
-            dims = (((1,), (side,)), ((), ()))
+    def sweep(values, which, side, part, begin, end):
+        dims = (((1,), (side,)), ((), ()))
+
+        def one_slot(s, carry):
+            index = slots[s, which]
             wide = lax.dot_general(values[index], t_high[s], dims, preferred_element_type=F32)
             rest = lax.dot_general(values[index, :bottom], t_low[s], dims,
                                    preferred_element_type=F32)
             part[s, :rhs] = wide[:rhs] + (wide[bottom:] + rest[:rhs])
             part[s, rhs:] = wide[rhs:rhs + EXTRA] + rest[rhs:rhs + EXTRA]
-        return carry
+            return carry
+
+        lax.fori_loop(begin, end, one_slot, 0)
 
     def column_image(b, span):
         total = col_part[where_slot[b], span]
@@ -329,85 +326,102 @@
 
     for repeat in range(ITERS):
         first = repeat == 0
-        if first:
-            def ready_row(b, carry):
-                put(x_row, b, v_row[0, b])
+        row_buf, col_buf = v_row.at[repeat], v_col.at[repeat]
+        parts = pieces(rhs + EXTRA, PIECE_FIRST) if first else pieces(rhs, PIECE)
+        if not first:
+            next(relay)
+            small_middle(sends_s, 0)
+            next(relay)
+        gather_cols(col_buf, v_parts, gv_col, hv_c)
+        weight = None
+        if not first:
+            norm_next = small_end(0)
+            weight = column(norm_next / norm_now, rhs, tile)
+            norm_now = norm_next
+            direction[...] = res_out[...] + weight * direction[...]
+
+        def ready(fresh, kept, target):
+            def one_block(b, carry):
+                value = fresh[repeat, b]
+                if repeat:
+                    value = value + weight * (fresh[0, b] if repeat == 1 else kept[b])
+                    kept[b] = value
+                put(target, b, value)
                 return carry
 
-            def ready_col(a, carry):
-                put(x_col, a, v_col[0, a])
-                return carry
-        else:
-            old_row = v_row.at[0] if repeat == 1 else d_row
-            old_col = v_col.at[0] if repeat == 1 else d_col
-            weight = column(beta, rhs, tile)
-
-            def ready_row(b, carry):
-                value = v_row[repeat, b] + weight * old_row[b]
-                d_row[b] = value
-                put(x_row, b, value)
-                return carry
-
-            def ready_col(a, carry):
-                value = v_col[repeat, a] + weight * old_col[a]
-                d_col[a] = value
-                put(x_col, a, value)
-                return carry
-
-        lax.fori_loop(0, rows, ready_row, 0)
-        lax.fori_loop(0, cols, ready_col, 0)
-        lax.fori_loop(0, count, sweep, 0)
-
+            return one_block
+
+        lax.fori_loop(0, cols, ready(v_col, d_col, x_col), 0)
+        sweep(x_col, 0, 0, col_part, 0, half)
+        for _ in relay:
+            pass
+        sweep(x_col, 0, 0, col_part, half, count)
         held_col = v_col.at[0] if first else d_col
         held_row = v_row.at[0] if first else d_row
-        parts = pieces(rhs + EXTRA, PIECE_FIRST) if first else pieces(rhs, PIECE)
         sends_r.drain()
-        sends_s.drain()
 
         def send_across(i):
             for j, side in enumerate(side_of):
                 for n, (start, size) in enumerate(parts):
                     span = pl.ds(start, size)
                     x_stage[i, j, span] = column_image(order[i] * inner + side, span)
-                    sends_r.go(remote(x_stage.at[i, j, span], x_got.at[i, j, span],
-                                      qx.at[i, j, n], rx.at[i, j, n], (z * inner + side, c)))
+                    sends_r.go(remote(x_stage.at[i, j, span], x_got.at[repeat, i, j, span],
+                                      qx.at[i, j, n], rx.at[repeat, i, j, n], (z * inner + side, c)))
 
         def joined(i, n, span):
             value = column_image(order[i] * inner + w, span)
             for j in range(inner - 1):
-                block = x_got.at[i, j, span]
-                remote(block, block, qx.at[i, j, n], rx.at[i, j, n],
+                block = x_got.at[repeat, i, j, span]
+                remote(block, block, qx.at[i, j, n], rx.at[repeat, i, j, n],
                        (z * inner + side_of[j], c)).wait_recv()
-                value = value + x_got[i, j, span]
+                value = value + x_got[repeat, i, j, span]
             return value
 
-        send_across(0)
-        own_err = errors[...] if first else diag[...]
+        for i in range(outer):
+            send_across(i)
+        gather_rows(row_buf, v_parts, gv_row, hv_x)
+        if first:
+            norm_now = small_end(0)
+            sends_f.drain()
+        lax.fori_loop(0, rows, ready(v_row, d_row, x_row), 0)
+        sends_s.drain()
         here = direction[...]
-        dots = fold(own_err * here * here)
+        dots = fold((errors[...] if first else diag[...]) * here * here)
+        if first:
+            sweep(x_row, 1, 1, row_part, 0, count)
+            extra = pl.ds(rhs, EXTRA)
+
+            def weigh(b, carry):
+                held = held_row[b]
+                return carry + fold(column_image(b, extra)[:1] * (held * held))
+
+            dots = lax.fori_loop(0, rows, weigh, dots)
+
+            def weigh_col(a, carry):
+                held = held_col[a]
+                return carry + fold(row_image(a, extra)[:1] * (held * held))
+
+            dots = lax.fori_loop(0, cols, weigh_col, dots)
+
+        def meet(b, carry):
+            return carry + 2.0 * fold(column_image(b, pl.ds(0, rhs)) * held_row[b])
+
+        dots = lax.fori_loop(0, rows, meet, dots)
+        small_start(sends_s, 1, lane_sums(dots))
+        if not first:
+            sweep(x_row, 1, 1, row_part, 0, half)
+            small_middle(sends_s, 1)
+            sweep(x_row, 1, 1, row_part, half, count)
         for k in range(cols):
             a = to_col[k][1] if k < cols - 1 else c
             for n, (start, size) in enumerate(parts):
                 span = pl.ds(start, size)
-                value = row_image(a, span)
-                c_stage[k, span] = value
+                c_stage[k, span] = row_image(a, span)
                 if k < cols - 1:
                     sends_r.go(remote(c_stage.at[k, span], c_got.at[k, span],
                                       qc.at[k, n], rc.at[k, n], to_col[k]))
-            held = held_col[a]
-            dots = dots + 2.0 * fold(c_stage[k, :rhs] * held)
-            if first:
-                dots = dots + fold(c_stage[k, rhs:rhs + 1] * (held * held))
         if first:
-            def weigh(b, carry):
-                held = held_row[b]
-                return carry + fold(column_image(b, pl.ds(rhs, EXTRA))[:1] * (held * held))
-
-            dots = lax.fori_loop(0, rows, weigh, dots)
-        small_start(sends_s, 1, lane_sums(dots))
-        for i in range(1, outer):
-            send_across(i)
-        small_middle(sends_s, 1)
+            small_middle(sends_s, 1)
 
         for i in range(outer - 1):
             q = order[i]
@@ -456,20 +470,11 @@
             v_row[repeat + 1, r] = residual
             v_col[repeat + 1, c] = residual
             row_buf, col_buf = v_row.at[repeat + 1], v_col.at[repeat + 1]
+            sends_s.drain()
+            small_start(sends_s, 0, lane_sums(fold(residual * residual)))
             gather_start(sends_v, row_buf.at[r], row_buf, col_buf, v_parts,
                          gv_row, gv_col, hv_z, hv_x, hv_c)
-            sends_s.drain()
-            small_start(sends_s, 0, lane_sums(fold(residual * residual)))
             relay = gather_relay(sends_v, row_buf, v_parts, gv_row, hv_z, hv_x)
-            next(relay)
-            small_middle(sends_s, 0)
-            for _ in relay:
-                pass
-            gather_finish(row_buf, col_buf, v_parts, gv_row, gv_col, hv_x, hv_c)
-            norm_next = small_end(0)
-            beta = norm_next / norm_now
-            norm_now = norm_next
-            direction[...] = residual + column(beta, rhs, tile) * here
     sends_r.drain()
     sends_s.drain()
     sends_v.drain()
@@ -505,7 +510,7 @@
         pltpu.VMEM((2, cols, 8, 128), F32),
         pltpu.VMEM((2, rows, 8, 128), F32),
         pltpu.VMEM((outer, sides, wide, tile), F32),
-        pltpu.VMEM((outer, sides, wide, tile), F32),
+        pltpu.VMEM((ITERS, outer, sides, wide, tile), F32),
         pltpu.VMEM((outer, wide, tile), F32),
         pltpu.VMEM((2, outer, wide, tile), F32),
         pltpu.VMEM((cols, wide, tile), F32),
@@ -516,7 +521,7 @@
         dma((rows, nf)), dma((cols, nf)), dma((rows, nv)), dma((cols, nv)),
         dma((2, outer, nf)), dma((2, outer, sides, nf)), dma((cols, nf)),
         dma((2, outer, nv)), dma((2, outer, sides, nv)), dma((cols, nv)),
-        dma((outer, sides, nr)), dma((2, outer, nr)), dma((cols, nr)),
+        dma((ITERS, outer, sides, nr)), dma((2, outer, nr)), dma((cols, nr)),
         dma((outer, sides, nr)), dma((outer, nr)), dma((cols, nr)),
         dma((2, cols)), dma((2, rows)), dma((2, cols)), dma((2, rows)),
     ]

time: 152 us -> 131 us (0.86)
  Pallas kernels: 147 us -> 127 us
    pallas_call x1, Pallas kernels: 147 us -> 127 us  [shards(): pl.pallas_call(functools.partial(kernel, rows, cols), out_shape=(out, out...]
where the time goes in v2:
time: 131 us
  Pallas kernels  127 us (97%)
  local copies, waits for them, and re-layouts  3.61 us (3%)
    pallas_call x1, Pallas kernels, shards(): pl.pallas_call(functools.partial(kernel, rows, cols), out_shape=(out, out...  127 us
    unnamed x6, local copies, waits for them, and re-layouts  2.94 us

profile of v2, /device:TPU:0, one launch (start us, length us, event | category | flops | bytes accessed | tf_op | source)
XLA Modules:
  0.0 131.3 jit_solution(248427919786083089)
XLA Ops:
  0.6 0.0 copy-start.1
  0.6 0.7 copy-done.1
  1.3 0.7 copy.9
  2.0 127.0 %shard_map.77 = (f32[64,512]{1,0:T(8,128)}, f32[64,512]{1,0:T(8,128)}) custom-call(f32[64,512]{1,0:T(8,128)} %innov.1, f32[64,512]{1,0:T(8,128)} %factors.1, s32[1,512]{1,0:T(1,128)} %bitcast.4, f32[1,512]{1,0:T(1,128)} %bitcast.5, f32[2,2]{1,0:T(2,128)} %coupling.1, s32[8,3]{1,0:T(8,128)} %bitcast.3), custom_call_target="tpu_custom_call" | custom-call | tf_op jit(solution)/shard_map/pallas_call | solution.py:529
  129.0 0.0 copy-start
  129.0 1.6 %copy.12 = f32[64,512]{1,0:T(8,128)} copy(f32[64,512]{1,0:T(8,128)} %get-tuple-element.4) | data formatting | bytes 262144
  130.6 0.0 copy-done
  130.6 0.7 copy.13
Async XLA Ops:
  0.6 0.7 copy-start.1
  129.0 1.6 %copy-start = (f32[64,512]{1,0:T(8,128)S(1)}, f32[64,512]{1,0:T(8,128)}, u32[]{:S(2)}) copy-start(f32[64,512]{1,0:T(8,128)} %get-tuple-element.5) | copy-start | bytes 393220

commit v3 on v2

--- a/solution.py
+++ b/solution.py
@@ -15,8 +15,8 @@
 SMEM = pl.BlockSpec(memory_space=pltpu.SMEM)
 F32, BF16 = jnp.float32, jnp.bfloat16
 PIECE_FACTORS = 24
-PIECE_FIRST = 24
-PIECE = 16
+PIECE_FIRST = 40
+PIECE = 32
 EXTRA = 8
 ONES = 16
 DEAD = 1000.0
@@ -277,9 +277,9 @@
         return carry
 
     half = count // 2
-    lax.fori_loop(0, half, build, 0)
+    lax.fori_loop(0, half, build, 0, unroll=2)
     next(relay)
-    lax.fori_loop(half, count, build, 0)
+    lax.fori_loop(half, count, build, 0, unroll=2)
 
     ones_rows = jnp.ones((ONES, tile), BF16)
     bottom = rhs + ONES
@@ -302,7 +302,7 @@
             part[s, rhs:] = wide[rhs:rhs + EXTRA] + rest[rhs:rhs + EXTRA]
             return carry
 
-        lax.fori_loop(begin, end, one_slot, 0)
+        lax.fori_loop(begin, end, one_slot, 0, unroll=2)
 
     def column_image(b, span):
         total = col_part[where_slot[b], span]
@@ -377,6 +377,18 @@
                 value = value + x_got[repeat, i, j, span]
             return value
 
+        def home_steps():
+            for i in range(outer - 1):
+                q = order[i]
+                target = (q * inner + w, c)
+                for n, (start, size) in enumerate(parts):
+                    span = pl.ds(start, size)
+                    z_stage[i, span] = joined(i, n, span)
+                    sends_r.go(remote(z_stage.at[i, span], z_got.at[z, span],
+                                      qz.at[i, n], rz.at[z, n], target))
+                yield i
+
+        homeward = home_steps()
         for i in range(outer):
             send_across(i)
         gather_rows(row_buf, v_parts, gv_row, hv_x)
@@ -411,7 +423,9 @@
         if not first:
             sweep(x_row, 1, 1, row_part, 0, half)
             small_middle(sends_s, 1)
+            next(homeward)
             sweep(x_row, 1, 1, row_part, half, count)
+            next(homeward)
         for k in range(cols):
             a = to_col[k][1] if k < cols - 1 else c
             for n, (start, size) in enumerate(parts):
@@ -423,24 +437,8 @@
         if first:
             small_middle(sends_s, 1)
 
-        for i in range(outer - 1):
-            q = order[i]
-            below = q < z
-            way = jnp.where(below, 0, 1)
-            more = jnp.where(below, z + 1 < outer, z > 0)
-            target = (jnp.where(below, r - inner, r + inner), c)
-            for n, (start, size) in enumerate(parts):
-                span = pl.ds(start, size)
-                z_stage[i, span] = joined(i, n, span)
-                copy = remote(z_stage.at[i, span], z_got.at[way, q, span],
-                              qz.at[i, n], rz.at[way, q, n], target)
-
-                @pl.when(more)
-                def _():
-                    copy.wait_recv()
-                    z_stage[i, span] += z_got[way, q, span]
-
-                sends_r.go(copy)
+        for _ in homeward:
+            pass
         for n, (start, size) in enumerate(parts):
             span = pl.ds(start, size)
             for k, q in enumerate(from_col):
@@ -450,13 +448,10 @@
             for k in range(cols - 1):
                 value = value + c_got[k, span]
             product[span] = value + joined(outer - 1, n, span)
-            for way, there in enumerate((has_high, has_low)):
-                @pl.when(there)
-                def _():
-                    block = z_got.at[way, z, span]
-                    remote(block, block, qz.at[0, n], rz.at[way, z, n],
-                           high if way == 0 else low).wait_recv()
-                    product[span] += z_got[way, z, span]
+            for i in range(outer - 1):
+                block = z_got.at[order[outer - 2 - i], span]
+                remote(block, block, qz.at[i, n], rz.at[order[outer - 2 - i], n], low).wait_recv()
+                product[span] += z_got[order[outer - 2 - i], span]
         alpha = norm_now / small_end(1)
         step = column(alpha, rhs, tile)
         if first:
@@ -512,7 +507,7 @@
         pltpu.VMEM((outer, sides, wide, tile), F32),
         pltpu.VMEM((ITERS, outer, sides, wide, tile), F32),
         pltpu.VMEM((outer, wide, tile), F32),
-        pltpu.VMEM((2, outer, wide, tile), F32),
+        pltpu.VMEM((outer, wide, tile), F32),
         pltpu.VMEM((cols, wide, tile), F32),
         pltpu.VMEM((cols, wide, tile), F32),
         pltpu.VMEM((wide, tile), F32),
@@ -521,7 +516,7 @@
         dma((rows, nf)), dma((cols, nf)), dma((rows, nv)), dma((cols, nv)),
         dma((2, outer, nf)), dma((2, outer, sides, nf)), dma((cols, nf)),
         dma((2, outer, nv)), dma((2, outer, sides, nv)), dma((cols, nv)),
-        dma((ITERS, outer, sides, nr)), dma((2, outer, nr)), dma((cols, nr)),
+        dma((ITERS, outer, sides, nr)), dma((outer, nr)), dma((cols, nr)),
         dma((outer, sides, nr)), dma((outer, nr)), dma((cols, nr)),
         dma((2, cols)), dma((2, rows)), dma((2, cols)), dma((2, rows)),
     ]

time: 131 us -> 122 us (0.931)
  Pallas kernels: 127 us -> 118 us
    pallas_call x1, Pallas kernels: 127 us -> 118 us  [shards(): pl.pallas_call(functools.partial(kernel, rows, cols), out_shape=(out, out...]
where the time goes in v3:
time: 122 us
  Pallas kernels  118 us (97%)
  local copies, waits for them, and re-layouts  3.61 us (3%)
    pallas_call x1, Pallas kernels, shards(): pl.pallas_call(functools.partial(kernel, rows, cols), out_shape=(out, out...  118 us
    unnamed x6, local copies, waits for them, and re-layouts  2.94 us

profile of v3, /device:TPU:0, one launch (start us, length us, event | category | flops | bytes accessed | tf_op | source)
XLA Modules:
  0.0 122.3 jit_solution(2137553313776642118)
XLA Ops:
  0.6 0.0 copy-start.1
  0.6 0.7 copy-done.1
  1.3 0.7 copy.9
  2.0 118.0 %shard_map.77 = (f32[64,512]{1,0:T(8,128)}, f32[64,512]{1,0:T(8,128)}) custom-call(f32[64,512]{1,0:T(8,128)} %innov.1, f32[64,512]{1,0:T(8,128)} %factors.1, s32[1,512]{1,0:T(1,128)} %bitcast.4, f32[1,512]{1,0:T(1,128)} %bitcast.5, f32[2,2]{1,0:T(2,128)} %coupling.1, s32[8,3]{1,0:T(8,128)} %bitcast.3), custom_call_target="tpu_custom_call" | custom-call | tf_op jit(solution)/shard_map/pallas_call | solution.py:524
  120.0 0.0 copy-start
  120.0 1.6 %copy.12 = f32[64,512]{1,0:T(8,128)} copy(f32[64,512]{1,0:T(8,128)} %get-tuple-element.4) | data formatting | bytes 262144
  121.6 0.0 copy-done
  121.6 0.7 copy.13
Async XLA Ops:
  0.6 0.7 copy-start.1
  120.0 1.6 %copy-start = (f32[64,512]{1,0:T(8,128)S(1)}, f32[64,512]{1,0:T(8,128)}, u32[]{:S(2)}) copy-start(f32[64,512]{1,0:T(8,128)} %get-tuple-element.5) | copy-start | bytes 393220
